TPU v7x, 8 devices: a whole 2x2x1 slice. The times are simulated.
8 devices in a mesh: dp: 1 (over z), cp: 8 (over y, x, core).
Axes of the slice: x: 2, y: 2, z: 1, core: 2. Of those that a mesh axis runs over, the one named last changes fastest.
Arguments:
- x: bfloat16 [2048, 3584], P(('dp', 'cp'))
- seg: int32 [2048], P(('dp', 'cp'))
- wq: bfloat16 [3584, 3584], replicated
- wk: bfloat16 [3584, 512], replicated
- wv: bfloat16 [3584, 512], replicated
- wo: bfloat16 [3584, 3584], replicated
Outputs:
- output: bfloat16 [2048, 3584], P(('dp', 'cp'))
All inputs are finite; a program needn't handle non-finite values.
Results may differ from a plain program's by a relative error of at most 0.00752571.
Values are sent between devices in bfloat16 or wider.
A program may use at most 1 GiB of HBM per device.

v0:
```python
import functools

import jax
import jax.numpy as jnp
from jax import lax
from jax.experimental import pallas as pl
from jax.experimental.pallas import tpu as pltpu
from jax.sharding import PartitionSpec as P

DH = 128
HALF = 128
KB = 256
NC = 512
MESH = pl.DeviceIdType.MESH
F32 = jnp.float32
BF16 = jnp.bfloat16
LOG2E = 1.4426950408889634


def _kernel(n, g_sz, x_hbm, seg_hbm, wq_hbm, wk_hbm, wv_hbm, wo_hbm, y_hbm,
            x_s, w_s, kv_s, q_s, o_s, s_s, b_s, m_s, l_s, a_s, y_s, yb_s, seg_s, sq_s,
            x_sem, w_sem, o_sem, ss_sem, sr_sem, send_sem, recv_sem, loc_sem):
    me = lax.axis_index("cp")
    c, xx, yy = me % 2, (me // 2) % 2, me // 4

    def dev(dy, dx, dc):
        ny = 1 - yy if dy else yy
        nx = 1 - xx if dx else xx
        nc = 1 - c if dc else c
        return ny * 4 + nx * 2 + nc

    d_model = x_s.shape[1]
    n_q = wq_hbm.shape[1] // NC
    n_kv = wk_hbm.shape[1] // DH
    half_k = d_model // 2
    peers = [dev(k // 4, (k // 2) % 2, k % 2) for k in range(n)]
    sib = peers[1]

    def load(i):
        if i < 2:
            cols = pl.ds(i * 2 * DH, 2 * DH)
            return [
                pltpu.make_async_copy(wk_hbm.at[:, cols], w_s.at[i, :, pl.ds(0, 2 * DH)], w_sem.at[i]),
                pltpu.make_async_copy(wv_hbm.at[:, cols], w_s.at[i, :, pl.ds(2 * DH, 2 * DH)], w_sem.at[n_q * 2 + 2 + i]),
            ]
        if i < 2 + n_q:
            return [pltpu.make_async_copy(wq_hbm.at[:, pl.ds((i - 2) * NC, NC)], w_s.at[i], w_sem.at[i])]
        j = i - 2 - n_q
        return [pltpu.make_async_copy(wo_hbm.at[:, pl.ds(j * NC, NC)], w_s.at[j], w_sem.at[i])]

    def start(i):
        for cp in load(i):
            cp.start()

    def wait(i):
        for cp in load(i):
            cp.wait()

    x_cp = pltpu.make_async_copy(x_hbm, x_s, x_sem)
    seg_cp = pltpu.make_async_copy(seg_hbm, seg_s.at[me], loc_sem)
    x_cp.start()
    seg_cp.start()
    start(0)
    start(1)
    start(2)

    barrier = pltpu.get_barrier_semaphore()
    for k in range(1, n):
        pl.semaphore_signal(barrier, inc=1, device_id={"cp": peers[k]}, device_id_type=MESH)
    pl.semaphore_wait(barrier, n - 1)

    def seg_copy(k):
        return pltpu.make_async_remote_copy(
            src_ref=seg_s.at[me], dst_ref=seg_s.at[me], send_sem=ss_sem.at[k], recv_sem=sr_sem.at[k],
            device_id={"cp": peers[k]}, device_id_type=MESH)

    def seg_recv(k):
        return pltpu.make_async_remote_copy(
            src_ref=seg_s.at[peers[k]], dst_ref=seg_s.at[peers[k]], send_sem=ss_sem.at[k], recv_sem=sr_sem.at[k],
            device_id={"cp": peers[k]}, device_id_type=MESH)

    seg_cp.wait()
    for k in range(1, n):
        seg_copy(k).start()

    own_to = [1, 2, 4, 6]

    def kv_copy(g, role, ab):
        src_dev = me if role < 4 else peers[own_to[role - 3]]
        to = peers[own_to[role]] if role < 4 else sib
        return _chunk(g, role, ab, src_dev, to)

    def kv_recv(g, role, ab):
        src_dev = peers[own_to[role]] if role < 4 else peers[own_to[role - 3] + 1]
        return _chunk(g, role, ab, src_dev, sib)

    def _chunk(g, role, ab, src_dev, to):
        piece = src_dev if ab == 0 else 2 * n - 1 - src_dev
        rows = pl.ds(pl.multiple_of(piece * HALF, HALF), HALF)
        ref = kv_s.at[g, :, rows, :]
        return pltpu.make_async_remote_copy(
            src_ref=ref, dst_ref=ref, send_sem=send_sem.at[g, role, ab], recv_sem=recv_sem.at[g, role, ab],
            device_id={"cp": to}, device_id_type=MESH)

    x_cp.wait()
    for i in range(2):
        wait(i)
        start(3 + i)
        r = jnp.dot(x_s[...], w_s[i], preferred_element_type=F32).astype(BF16)
        for gg in range(2):
            for ab in range(2):
                piece = me if ab == 0 else 2 * n - 1 - me
                rows = pl.ds(pl.multiple_of(piece * HALF, HALF), HALF)
                for t in range(2):
                    lo = t * 2 * DH + gg * DH
                    kv_s[2 * i + gg, t, rows, :] = r[ab * HALF:(ab + 1) * HALF, lo:lo + DH]
        start(2 + n_q + i)
        for gg in range(2):
            for ab in range(2):
                for role in range(4):
                    kv_copy(2 * i + gg, role, ab).start()

    def q_chunk(j):
        r = jnp.dot(x_s[...], w_s[2 + j], preferred_element_type=F32).astype(BF16)
        for hh in range(NC // DH):
            for ab in range(2):
                q_s[ab, j * (NC // DH) + hh] = r[ab * HALF:(ab + 1) * HALF, hh * DH:(hh + 1) * DH]

    for j in range(n_q):
        wait(2 + j)
        if 5 + j < 2 + n_q:
            start(5 + j)
        q_chunk(j)
        if 2 + j < n_q:
            start(4 + n_q + j)

    for k in range(1, n):
        seg_recv(k).wait_recv()
    n_a = me // 2 + 1
    n_t = n + 1
    for ab in range(2):
        row = seg_s[me, pl.ds(ab, 1), :]
        sq_s[ab] = jnp.transpose(jnp.broadcast_to(row, (HALF, HALF)))

    def block_of(t):
        ab = jnp.where(t >= n_a, 1, 0)
        return ab, t - ab * n_a

    def mask_step(t, _):
        ab, kb = block_of(t)
        qp = jnp.where(ab == 1, 2 * n - 1 - me, me)
        pos_q = qp * HALF + lax.broadcasted_iota(jnp.int32, (HALF, HALF), 0)
        for h in range(2):
            p = kb * 2 + h
            hi = jnp.where(p >= n, 1, 0)
            d = jnp.where(p >= n, 2 * n - 1 - p, p)
            sk = seg_s[d, pl.ds(hi, 1), :]
            pos_k = p * HALF + lax.broadcasted_iota(jnp.int32, (HALF, HALF), 1)
            ok = (sq_s[ab] == sk) & (pos_k <= pos_q)
            b_s[t, :, h * HALF:(h + 1) * HALF] = jnp.where(ok, 0.0, -jnp.inf)
        return 0

    lax.fori_loop(0, n_t, mask_step, 0)

    rows_g = g_sz * HALF
    scale = LOG2E * DH ** -0.5

    def attention(g):
        m_s[...] = jnp.full_like(m_s, -jnp.inf)

        def scores(t, _):
            ab, kb = block_of(t)
            q = q_s[ab, pl.ds(g * g_sz, g_sz)].reshape(rows_g, DH)
            k = kv_s[g, 0, pl.ds(pl.multiple_of(kb * KB, KB), KB), :]
            s = lax.dot_general(q, k, (((1,), (1,)), ((), ())), preferred_element_type=F32)
            s = s.reshape(g_sz, HALF, KB)
            for j in range(g_sz):
                sj = s[j] + b_s[t]
                s_s[t, j] = sj
                m_s[ab, j] = jnp.maximum(m_s[ab, j], jnp.maximum(sj[:, :HALF], sj[:, HALF:]))
            return 0

        lax.fori_loop(0, n_t, scores, 0)
        for ab in range(2):
            for j in range(g_sz):
                m_s[ab, j] = jnp.broadcast_to(jnp.max(m_s[ab, j], axis=1, keepdims=True), (HALF, HALF))
        l_s[...] = jnp.zeros_like(l_s)
        a_s[...] = jnp.zeros_like(a_s)

        def values(t, _):
            ab, kb = block_of(t)
            v = kv_s[g, 1, pl.ds(pl.multiple_of(kb * KB, KB), KB), :]
            ps = []
            for j in range(g_sz):
                m = m_s[ab, j]
                p0 = jnp.exp2((s_s[t, j, :, :HALF] - m) * scale)
                p1 = jnp.exp2((s_s[t, j, :, HALF:] - m) * scale)
                l_s[ab, j] += p0 + p1
                ps.append(jnp.concatenate([p0.astype(BF16), p1.astype(BF16)], axis=1))
            p = jnp.concatenate(ps, axis=0)
            a_s[ab] += jnp.dot(p, v, preferred_element_type=F32).reshape(g_sz, HALF, DH)
            return 0

        lax.fori_loop(0, n_t, values, 0)
        for ab in range(2):
            for j in range(g_sz):
                l = jnp.sum(l_s[ab, j], axis=1, keepdims=True)
                o = (a_s[ab, j] / l).astype(BF16)
                cols = pl.ds(pl.multiple_of((g * g_sz + j) * DH, DH), DH)
                o_s[ab * HALF:(ab + 1) * HALF, cols] = o

    def pass_on(g):
        for role in (1, 2, 3):
            for ab in range(2):
                kv_recv(g, role, ab).wait_recv()
                kv_copy(g, role + 3, ab).start()

    def arrived(g):
        for role in (0, 4, 5, 6):
            for ab in range(2):
                kv_recv(g, role, ab).wait_recv()

    pass_on(0)
    for hf in range(2):
        for gg in range(2):
            g = hf * 2 + gg
            if g + 1 < n_kv:
                pass
            arrived(g)
            attention(g)
            if g + 1 < n_kv:
                pass_on(g + 1)

        def out_chunk(j, _):
            o = o_s[:, hf * half_k:(hf + 1) * half_k]
            y = jnp.dot(o, w_s[j, hf * half_k:(hf + 1) * half_k, :], preferred_element_type=F32)
            if hf == 0:
                y_s[j] = y
            else:
                yb_s[j] = (y_s[j] + y).astype(BF16)
            return 0

        for j in range(n_q):
            if hf == 0:
                wait(2 + n_q + j)
            out_chunk(j, 0)
            if hf == 1:
                pltpu.make_async_copy(yb_s.at[j], y_hbm.at[:, pl.ds(j * NC, NC)], o_sem.at[j]).start()

    for j in range(n_q):
        pltpu.make_async_copy(yb_s.at[j], y_hbm.at[:, pl.ds(j * NC, NC)], o_sem.at[j]).wait()
    for k in range(1, n):
        seg_copy(k).wait_send()
    for g in range(n_kv):
        for role in range(7):
            for ab in range(2):
                kv_copy(g, role, ab).wait_send()


def solution(mesh):
    n = mesh.shape["cp"]

    def local(x, seg, wq, wk, wv, wo):
        lq, d = x.shape
        hq = wq.shape[1] // DH
        hkv = wk.shape[1] // DH
        g_sz = hq // hkv
        n_q = wq.shape[1] // NC
        dma = pltpu.SemaphoreType.DMA
        anyspec = pl.BlockSpec(memory_space=pl.ANY)
        return pl.pallas_call(
            functools.partial(_kernel, n, g_sz),
            out_shape=jax.ShapeDtypeStruct((lq, wo.shape[1]), BF16),
            in_specs=[anyspec] * 6,
            out_specs=anyspec,
            scratch_shapes=[
                pltpu.VMEM((lq, d), BF16),
                pltpu.VMEM((n_q + 2, d, NC), BF16),
                pltpu.VMEM((hkv, 2, n * lq, DH), BF16),
                pltpu.VMEM((2, hq, HALF, DH), BF16),
                pltpu.VMEM((lq, hq * DH), BF16),
                pltpu.VMEM((n + 1, g_sz, HALF, KB), F32),
                pltpu.VMEM((n + 1, HALF, KB), F32),
                pltpu.VMEM((2, g_sz, HALF, HALF), F32),
                pltpu.VMEM((2, g_sz, HALF, HALF), F32),
                pltpu.VMEM((2, g_sz, HALF, DH), F32),
                pltpu.VMEM((n_q, lq, NC), F32),
                pltpu.VMEM((n_q, lq, NC), BF16),
                pltpu.VMEM((n, 2, HALF), jnp.int32),
                pltpu.VMEM((2, HALF, HALF), jnp.int32),
                dma, dma((2 * n_q + 4,)), dma((n_q,)), dma((n,)), dma((n,)),
                dma((hkv, 7, 2)), dma((hkv, 7, 2)), dma,
            ],
            compiler_params=pltpu.CompilerParams(
                collective_id=0, has_side_effects=True, vmem_limit_bytes=67043328),
            name="layer",
        )(x, seg.reshape(2, HALF), wq, wk, wv, wo)

    rows = P(("dp", "cp"), None)
    return jax.shard_map(local, mesh=mesh, in_specs=(rows, P(("dp", "cp")), P(), P(), P(), P()), out_specs=rows, check_vma=False)
```

profile of v0, /device:TPU:0, one launch (start us, length us, event | category | flops | bytes accessed | tf_op | source)
XLA Modules:
  0.0 60.7 jit_solution(2815534275079922486)
XLA Ops:
  0.0 57.8 %layer.1 = bf16[256,3584]{1,0:T(8,128)(2,1)} custom-call(bf16[256,3584]{1,0:T(8,128)(2,1)} %x_hbm.1, s32[2,128]{1,0:T(2,128)} %bitcast.1, bf16[3584,3584]{1,0:T(8,128)(2,1)} %wq_hbm.1, bf16[3584,512]{1,0:T(8,128)(2,1)} %wk_hbm.1, bf16[3584,512]{1,0:T(8,128)(2,1)} %wv_hbm.1, bf16[3584,3584]{1,0:T(8,128)(2,1)} %wo_hbm.1), custom_call_target="tpu_custom_call" | custom-call | tf_op jit(solution)/shard_map/layer/pallas_call | solution.py:271
  57.8 2.8 %copy.8 = bf16[256,3584]{1,0:T(8,128)(2,1)} copy(bf16[256,3584]{1,0:T(8,128)(2,1)} %layer.1) | data formatting | bytes 3670016
where the time goes:
time: 60.8 us; the launch traced here: 60.7 us
  Pallas kernels  57.8 us (95%)
  local copies, waits for them, and re-layouts  2.85 us (5%)
    pallas_call x1, Pallas kernels, local(): pl.pallas_call(functools.partial(_kernel, n, g_sz), out_shape=jax.ShapeDt...  57.8 us
    unnamed x1, local copies, waits for them, and re-layouts  2.85 us

commit v1 on v0

v1 whole, which is shorter than its diff:
```python
import functools

import jax
import jax.numpy as jnp
from jax import lax
from jax.experimental import pallas as pl
from jax.experimental.pallas import tpu as pltpu
from jax.sharding import PartitionSpec as P

DH = 128
HALF = 128
KB = 256
NC = 512
MESH = pl.DeviceIdType.MESH
F32 = jnp.float32
BF16 = jnp.bfloat16
UNROLL = 3
LOG2E = 1.4426950408889634


def _kernel(n, g_sz, x_hbm, seg_hbm, wq_hbm, wk_hbm, wv_hbm, wo_hbm, y_hbm,
            x_s, w_s, kv_s, q_s, o_s, s_s, b_s, m_s, l_s, a_s, y_s, yb_s, seg_s,
            x_sem, w_sem, o_sem, ss_sem, sr_sem, send_sem, recv_sem, loc_sem):
    me = lax.axis_index("cp")
    c, xx, yy = me % 2, (me // 2) % 2, me // 4

    def dev(dy, dx, dc):
        ny = 1 - yy if dy else yy
        nx = 1 - xx if dx else xx
        nc = 1 - c if dc else c
        return ny * 4 + nx * 2 + nc

    d_model = x_s.shape[1]
    n_q = wq_hbm.shape[1] // NC
    n_kv = wk_hbm.shape[1] // DH
    half_k = d_model // 2
    peers = [dev(k // 4, (k // 2) % 2, k % 2) for k in range(n)]
    sib = peers[1]

    def load(i):
        if i < 2:
            cols = pl.ds(i * 2 * DH, 2 * DH)
            return [
                pltpu.make_async_copy(wk_hbm.at[:, cols], w_s.at[i, :, pl.ds(0, 2 * DH)], w_sem.at[i]),
                pltpu.make_async_copy(wv_hbm.at[:, cols], w_s.at[i, :, pl.ds(2 * DH, 2 * DH)], w_sem.at[n_q * 2 + 2 + i]),
            ]
        if i < 2 + n_q:
            return [pltpu.make_async_copy(wq_hbm.at[:, pl.ds((i - 2) * NC, NC)], w_s.at[i], w_sem.at[i])]
        j = i - 2 - n_q
        return [pltpu.make_async_copy(wo_hbm.at[:, pl.ds(j * NC, NC)], w_s.at[j], w_sem.at[i])]

    def start(i):
        for cp in load(i):
            cp.start()

    def wait(i):
        for cp in load(i):
            cp.wait()

    x_cp = pltpu.make_async_copy(x_hbm, x_s, x_sem)
    seg_cp = pltpu.make_async_copy(seg_hbm, seg_s.at[me], loc_sem)
    x_cp.start()
    seg_cp.start()
    start(0)
    start(1)
    start(2)

    def seg_copy(k):
        return pltpu.make_async_remote_copy(
            src_ref=seg_s.at[me], dst_ref=seg_s.at[me], send_sem=ss_sem.at[k], recv_sem=sr_sem.at[k],
            device_id={"cp": peers[k]}, device_id_type=MESH)

    def seg_recv(k):
        return pltpu.make_async_remote_copy(
            src_ref=seg_s.at[peers[k]], dst_ref=seg_s.at[peers[k]], send_sem=ss_sem.at[k], recv_sem=sr_sem.at[k],
            device_id={"cp": peers[k]}, device_id_type=MESH)

    barrier = pltpu.get_barrier_semaphore()
    for k in range(1, n):
        pl.semaphore_signal(barrier, inc=1, device_id={"cp": peers[k]}, device_id_type=MESH)

    own_to = [1, 2, 4, 6]

    def kv_copy(g, role, ab):
        if role < 3:
            src_dev, to = me, peers[own_to[role]]
        elif role == 3:
            src_dev, to = (peers[2], peers[4]) if ab == 0 else (peers[4], peers[2])
        else:
            src_dev, to = peers[own_to[role - 3]], sib
        return _chunk(g, role, ab, src_dev, to)

    def kv_recv(g, role, ab):
        src_dev = peers[own_to[role]] if role < 4 else peers[own_to[role - 3] + 1]
        return _chunk(g, role, ab, src_dev, sib)

    def _chunk(g, role, ab, src_dev, to):
        ref = kv_s.at[g, src_dev if ab == 0 else 2 * n - 1 - src_dev]
        return pltpu.make_async_remote_copy(
            src_ref=ref, dst_ref=ref, send_sem=send_sem.at[g, role, ab], recv_sem=recv_sem.at[g, role, ab],
            device_id={"cp": to}, device_id_type=MESH)

    def send_own(g):
        for role in (1, 2, 0):
            for ab in range(2):
                kv_copy(g, role, ab).start()

    def forward(g):
        for ab in range(2):
            for role in (1, 2):
                kv_recv(g, role, ab).wait_recv()
        for ab in range(2):
            kv_copy(g, 3, ab).start()
        for ab in range(2):
            for role in (4, 5):
                kv_copy(g, role, ab).start()

    def forward_diag(g):
        for ab in range(2):
            kv_recv(g, 3, ab).wait_recv()
        for ab in range(2):
            kv_copy(g, 6, ab).start()

    def arrived(g):
        for role in (0, 4, 5, 6):
            for ab in range(2):
                kv_recv(g, role, ab).wait_recv()

    x_cp.wait()
    for i in range(2):
        wait(i)
        start(3 + i)
        r = jnp.dot(x_s[...], w_s[i], preferred_element_type=F32)
        for gg in range(2):
            for ab in range(2):
                piece = me if ab == 0 else 2 * n - 1 - me
                part = r[ab * HALF:(ab + 1) * HALF]
                kv_s[2 * i + gg, piece, 0] = part[:, gg * DH:(gg + 1) * DH].astype(BF16)
                v = part[:, (2 + gg) * DH:(3 + gg) * DH]
                kv_s[2 * i + gg, piece, 1] = jnp.transpose(v).astype(BF16)
        if i == 0:
            pl.semaphore_wait(barrier, n - 1)
            send_own(0)
            send_own(1)
            seg_cp.wait()
            for k in range(1, n):
                seg_copy(k).start()

    def q_chunk(j):
        r = jnp.dot(x_s[...], w_s[2 + j], preferred_element_type=F32).astype(BF16)
        for hh in range(NC // DH):
            for ab in range(2):
                q_s[ab, j * (NC // DH) + hh] = r[ab * HALF:(ab + 1) * HALF, hh * DH:(hh + 1) * DH]

    for j in range(n_q):
        wait(2 + j)
        start(5 + j)
        q_chunk(j)
        if j == 2:
            forward(0)
            send_own(2)
        if j == 5:
            forward(1)
            send_own(3)
        if j == 6:
            forward_diag(0)
    for j in range(5 + n_q, 2 + 2 * n_q):
        start(j)

    for k in range(1, n):
        seg_recv(k).wait_recv()
    n_a = me // 2 + 1
    n_t = n + 1
    def block_of(t):
        ab = jnp.where(t >= n_a, 1, 0)
        return ab, t - ab * n_a

    def mask_step(t, _):
        ab, kb = block_of(t)
        qp = jnp.where(ab == 1, 2 * n - 1 - me, me)
        sq = seg_s[me, pl.ds(ab, 1), :]
        pos_q = qp * HALF + lax.broadcasted_iota(jnp.int32, (HALF, HALF), 1)
        for h in range(2):
            p = kb * 2 + h
            hi = jnp.where(p >= n, 1, 0)
            d = jnp.where(p >= n, 2 * n - 1 - p, p)
            sk = jnp.transpose(jnp.broadcast_to(seg_s[d, pl.ds(hi, 1), :], (HALF, HALF)))
            pos_k = p * HALF + lax.broadcasted_iota(jnp.int32, (HALF, HALF), 0)
            ok = (sk == sq) & (pos_k <= pos_q)
            b_s[t, h * HALF:(h + 1) * HALF, :] = jnp.where(ok, 0.0, -jnp.inf)
        return 0

    lax.fori_loop(0, n_t, mask_step, 0)

    rows_g = g_sz * HALF
    scale = LOG2E * DH ** -0.5
    sub = KB // 8

    def fold(op, a):
        return op(a.reshape(sub, 8, HALF), axis=0)

    def attention(g):
        m_s[...] = jnp.full_like(m_s, -jnp.inf)
        l_s[...] = jnp.zeros_like(l_s)
        a_s[...] = jnp.zeros_like(a_s)

        def scores(t):
            ab, kb = block_of(t)
            q = q_s[ab, pl.ds(g * g_sz, g_sz)].reshape(rows_g, DH)
            k = kv_s[g, pl.ds(kb * 2, 2), 0].reshape(KB, DH)
            s = lax.dot_general(k, q, (((1,), (1,)), ((), ())), preferred_element_type=F32)
            for j in range(g_sz):
                sj = s[:, j * HALF:(j + 1) * HALF] + b_s[t]
                s_s[t, j] = sj
                m_s[ab, j] = jnp.maximum(m_s[ab, j], fold(jnp.max, sj))

        def values(t):
            ab, kb = block_of(t)
            v = jnp.concatenate([kv_s[g, kb * 2, 1], kv_s[g, kb * 2 + 1, 1]], axis=1)
            ps = []
            for j in range(g_sz):
                p = jnp.exp2((s_s[t, j].reshape(sub, 8, HALF) - m_s[ab, j][None]) * scale)
                l_s[ab, j] += jnp.sum(p, axis=0)
                ps.append(p.reshape(KB, HALF).astype(BF16))
            p = jnp.concatenate(ps, axis=1)
            a_s[ab] += jnp.dot(v, p, preferred_element_type=F32)

        def loop(f):
            def body(i, _):
                for u in range(UNROLL):
                    f(i * UNROLL + u)
                return 0
            lax.fori_loop(0, n_t // UNROLL, body, 0)

        loop(scores)
        m_s[...] = jnp.broadcast_to(jnp.max(m_s[...], axis=2, keepdims=True), m_s.shape)
        loop(values)
        for ab in range(2):
            for j in range(g_sz):
                l = jnp.sum(l_s[ab, j], axis=0, keepdims=True)
                o = jnp.transpose(a_s[ab, :, j * HALF:(j + 1) * HALF] / l).astype(BF16)
                o_s[ab * HALF:(ab + 1) * HALF, (g * g_sz + j) * DH:(g * g_sz + j + 1) * DH] = o

    for hf in range(2):
        for gg in range(2):
            g = hf * 2 + gg
            arrived(g)
            attention(g)
            if g == 0:
                forward(2)
                forward_diag(1)
            if g == 1:
                forward(3)

        for j in range(n_q):
            if hf == 0:
                wait(2 + n_q + j)
            o = o_s[:, hf * half_k:(hf + 1) * half_k]
            y = jnp.dot(o, w_s[j, hf * half_k:(hf + 1) * half_k, :], preferred_element_type=F32)
            if hf == 0:
                y_s[j] = y
                if j == 1:
                    forward_diag(2)
                if j == 4:
                    forward_diag(3)
            else:
                yb_s[j] = (y_s[j] + y).astype(BF16)
                pltpu.make_async_copy(yb_s.at[j], y_hbm.at[:, pl.ds(j * NC, NC)], o_sem.at[j]).start()

    for j in range(n_q):
        pltpu.make_async_copy(yb_s.at[j], y_hbm.at[:, pl.ds(j * NC, NC)], o_sem.at[j]).wait()
    for k in range(1, n):
        seg_copy(k).wait_send()
    for g in range(n_kv):
        for role in range(7):
            for ab in range(2):
                kv_copy(g, role, ab).wait_send()


def solution(mesh):
    n = mesh.shape["cp"]

    def local(x, seg, wq, wk, wv, wo):
        lq, d = x.shape
        hq = wq.shape[1] // DH
        hkv = wk.shape[1] // DH
        g_sz = hq // hkv
        n_q = wq.shape[1] // NC
        dma = pltpu.SemaphoreType.DMA
        anyspec = pl.BlockSpec(memory_space=pl.ANY)
        return pl.pallas_call(
            functools.partial(_kernel, n, g_sz),
            out_shape=jax.ShapeDtypeStruct((lq, wo.shape[1]), BF16),
            in_specs=[anyspec] * 6,
            out_specs=anyspec,
            scratch_shapes=[
                pltpu.VMEM((lq, d), BF16),
                pltpu.VMEM((n_q + 2, d, NC), BF16),
                pltpu.VMEM((hkv, 2 * n, 2, HALF, DH), BF16),
                pltpu.VMEM((2, hq, HALF, DH), BF16),
                pltpu.VMEM((lq, hq * DH), BF16),
                pltpu.VMEM((n + 1, g_sz, KB, HALF), F32),
                pltpu.VMEM((n + 1, KB, HALF), F32),
                pltpu.VMEM((2, g_sz, 8, HALF), F32),
                pltpu.VMEM((2, g_sz, 8, HALF), F32),
                pltpu.VMEM((2, DH, g_sz * HALF), F32),
                pltpu.VMEM((n_q, lq, NC), F32),
                pltpu.VMEM((n_q, lq, NC), BF16),
                pltpu.VMEM((n, 2, HALF), jnp.int32),
                dma, dma((2 * n_q + 4,)), dma((n_q,)), dma((n,)), dma((n,)),
                dma((hkv, 7, 2)), dma((hkv, 7, 2)), dma,
            ],
            compiler_params=pltpu.CompilerParams(
                collective_id=0, has_side_effects=True, vmem_limit_bytes=67043328),
            name="layer",
        )(x, seg.reshape(2, HALF), wq, wk, wv, wo)

    rows = P(("dp", "cp"), None)
    return jax.shard_map(local, mesh=mesh, in_specs=(rows, P(("dp", "cp")), P(), P(), P(), P()), out_specs=rows, check_vma=False)
```

time: 60.8 us -> 49.7 us (0.82)
  Pallas kernels: 57.8 us -> 46.8 us
    pallas_call x1, Pallas kernels: 57.8 us -> 46.8 us  [local(): pl.pallas_call(functools.partial(_kernel, n, g_sz), out_shape=jax.ShapeDt...]
where the time goes in v1:
time: 49.7 us; the launch traced here: 49.6 us
  Pallas kernels  46.8 us (94%)
  local copies, waits for them, and re-layouts  2.85 us (6%)
    pallas_call x1, Pallas kernels, local(): pl.pallas_call(functools.partial(_kernel, n, g_sz), out_shape=jax.ShapeDt...  46.8 us
    unnamed x1, local copies, waits for them, and re-layouts  2.85 us

profile of v1, /device:TPU:0, one launch (start us, length us, event | category | flops | bytes accessed | tf_op | source)
XLA Modules:
  0.0 49.6 jit_solution(13684022187830228248)
XLA Ops:
  0.0 46.8 %layer.1 = bf16[256,3584]{1,0:T(8,128)(2,1)} custom-call(bf16[256,3584]{1,0:T(8,128)(2,1)} %x_hbm.1, s32[2,128]{1,0:T(2,128)} %bitcast.1, bf16[3584,3584]{1,0:T(8,128)(2,1)} %wq_hbm.1, bf16[3584,512]{1,0:T(8,128)(2,1)} %wk_hbm.1, bf16[3584,512]{1,0:T(8,128)(2,1)} %wv_hbm.1, bf16[3584,3584]{1,0:T(8,128)(2,1)} %wo_hbm.1), custom_call_target="tpu_custom_call" | custom-call | tf_op jit(solution)/shard_map/layer/pallas_call | solution.py:291
  46.8 2.8 %copy.8 = bf16[256,3584]{1,0:T(8,128)(2,1)} copy(bf16[256,3584]{1,0:T(8,128)(2,1)} %layer.1) | data formatting | bytes 3670016

commit v2 on v1

v2 whole, which is shorter than its diff:
```python
import functools

import jax
import jax.numpy as jnp
from jax import lax
from jax.experimental import pallas as pl
from jax.experimental.pallas import tpu as pltpu
from jax.sharding import PartitionSpec as P

DH = 128
HALF = 128
KB = 256
NC = 512
MESH = pl.DeviceIdType.MESH
F32 = jnp.float32
BF16 = jnp.bfloat16
LOG2E = 1.4426950408889634


def _kernel(n, g_sz, x_hbm, seg_hbm, wq_hbm, wk_hbm, wv_hbm, wo_hbm, y_ref,
            x_s, w_s, kv_s, q_s, o_s, s_s, b_s, m_s, l_s, a_s, ml_s, ll_s, al_s, y_s, seg_s,
            x_sem, w_sem, ss_sem, sr_sem, send_sem, rn_sem, rd_sem, rs_sem, loc_sem):
    me = lax.axis_index("cp")
    c, xx, yy = me % 2, (me // 2) % 2, me // 4

    def dev(dy, dx, dc):
        ny = 1 - yy if dy else yy
        nx = 1 - xx if dx else xx
        nc = 1 - c if dc else c
        return ny * 4 + nx * 2 + nc

    d_model = x_s.shape[1]
    n_q = wq_hbm.shape[1] // NC
    n_kv = wk_hbm.shape[1] // DH
    half_k = d_model // 2
    peers = [dev(k // 4, (k // 2) % 2, k % 2) for k in range(n)]
    sib = peers[1]

    def load(i):
        if i < 2:
            cols = pl.ds(i * 2 * DH, 2 * DH)
            return [
                pltpu.make_async_copy(wk_hbm.at[:, cols], w_s.at[i, :, pl.ds(0, 2 * DH)], w_sem.at[i]),
                pltpu.make_async_copy(wv_hbm.at[:, cols], w_s.at[i, :, pl.ds(2 * DH, 2 * DH)], w_sem.at[n_q * 2 + 2 + i]),
            ]
        if i < 2 + n_q:
            return [pltpu.make_async_copy(wq_hbm.at[:, pl.ds((i - 2) * NC, NC)], w_s.at[i], w_sem.at[i])]
        j = i - 2 - n_q
        return [pltpu.make_async_copy(wo_hbm.at[:, pl.ds(j * NC, NC)], w_s.at[j], w_sem.at[i])]

    def start(i):
        for cp in load(i):
            cp.start()

    def wait(i):
        for cp in load(i):
            cp.wait()

    x_cp = pltpu.make_async_copy(x_hbm, x_s, x_sem)
    seg_cp = pltpu.make_async_copy(seg_hbm, seg_s.at[me], loc_sem)
    x_cp.start()
    start(0)
    seg_cp.start()

    def seg_copy(k):
        return pltpu.make_async_remote_copy(
            src_ref=seg_s.at[me], dst_ref=seg_s.at[me], send_sem=ss_sem, recv_sem=sr_sem,
            device_id={"cp": peers[k]}, device_id_type=MESH)

    def seg_all():
        ref = seg_s.at[pl.ds(0, n - 1)]
        return pltpu.make_async_remote_copy(
            src_ref=ref, dst_ref=ref, send_sem=ss_sem, recv_sem=sr_sem,
            device_id={"cp": sib}, device_id_type=MESH)

    barrier = pltpu.get_barrier_semaphore()
    for k in range(1, n):
        pl.semaphore_signal(barrier, inc=1, device_id={"cp": peers[k]}, device_id_type=MESH)

    xn, yn, dg = peers[2], peers[4], peers[6]
    first, second = xn * (1 - c) + yn * c, yn * (1 - c) + xn * c

    def chunk(u, src_dev, to, recv):
        ab, g = u // n_kv, u % n_kv
        ref = kv_s.at[g, src_dev if ab == 0 else 2 * n - 1 - src_dev]
        return pltpu.make_async_remote_copy(
            src_ref=ref, dst_ref=ref, send_sem=send_sem, recv_sem=recv.at[u],
            device_id={"cp": to}, device_id_type=MESH)

    def wait_chunks(u, count, recv):
        ref = kv_s.at[u % n_kv, pl.ds(0, count)]
        pltpu.make_async_remote_copy(
            src_ref=ref, dst_ref=ref, send_sem=send_sem, recv_sem=recv.at[u],
            device_id={"cp": sib}, device_id_type=MESH).wait_recv()

    def own(u):
        chunk(u, me, xn, rn_sem).start()
        chunk(u, me, yn, rn_sem).start()
        chunk(u, me, sib, rs_sem).start()

    def forward(u):
        wait_chunks(u, 2, rn_sem)
        chunk(u, first, second, rd_sem).start()
        chunk(u, xn, sib, rs_sem).start()
        chunk(u, yn, sib, rs_sem).start()

    def diag(u):
        wait_chunks(u, 1, rd_sem)
        chunk(u, dg, sib, rs_sem).start()

    def arrived(u):
        wait_chunks(u, 4, rs_sem)

    def hook(name, *acts):
        with jax.named_scope(name):
            for act, u in acts:
                act(u)

    with jax.named_scope("wait_x"):
        x_cp.wait()
        start(1)
    for i in range(2):
        with jax.named_scope(f"wait_kv#i={i}"):
            wait(i)
            if i == 0:
                start(2)
            start(3 + i)
        with jax.named_scope(f"kv#i={i}"):
            r = jnp.dot(x_s[...], w_s[i], preferred_element_type=F32)
            for gg in range(2):
                for ab in range(2):
                    piece = me if ab == 0 else 2 * n - 1 - me
                    part = r[ab * HALF:(ab + 1) * HALF]
                    kv_s[2 * i + gg, piece, 0] = part[:, gg * DH:(gg + 1) * DH].astype(BF16)
                    v = part[:, (2 + gg) * DH:(3 + gg) * DH]
                    kv_s[2 * i + gg, piece, 1] = jnp.transpose(v).astype(BF16)
        if i == 0:
            with jax.named_scope("barrier"):
                pl.semaphore_wait(barrier, n - 1)
                own(0)
                own(1)
                seg_cp.wait()
                for k in range(1, n):
                    seg_copy(k).start()
        else:
            own(2)

    def q_chunk(j):
        r = jnp.dot(x_s[...], w_s[2 + j], preferred_element_type=F32).astype(BF16)
        for hh in range(NC // DH):
            for ab in range(2):
                q_s[ab, j * (NC // DH) + hh] = r[ab * HALF:(ab + 1) * HALF, hh * DH:(hh + 1) * DH]

    for j in range(n_q):
        with jax.named_scope(f"wait_q#j={j}"):
            wait(2 + j)
            start(5 + j)
        with jax.named_scope(f"q#j={j}"):
            q_chunk(j)
        if j == 2:
            hook("hookA", (forward, 0), (own, 3))
        if j == 4:
            hook("hookB", (forward, 1), (own, 4))
        if j == 5:
            hook("hookC", (diag, 0))
        if j == 6:
            hook("hookD", (forward, 2), (own, 5))
    for j in range(5 + n_q, 2 + 2 * n_q):
        start(j)

    n_l = n // 2
    n_h = n_l + 1
    n_a = me // 2 + 1

    def mixed(t):
        ab = jnp.where(t >= n_a, 1, 0)
        return ab, t + ab * (n_l - n_a)

    def mask_step(t, _):
        ab, kb = mixed(t - n_l)
        ab = jnp.where(t < n_l, 1, ab)
        kb = jnp.where(t < n_l, t, kb)
        qp = jnp.where(ab == 1, 2 * n - 1 - me, me)
        sq = seg_s[me, pl.ds(ab, 1), :]
        pos_q = qp * HALF + lax.broadcasted_iota(jnp.int32, (HALF, HALF), 1)
        for h in range(2):
            p = kb * 2 + h
            hi = jnp.where(p >= n, 1, 0)
            d = jnp.where(p >= n, 2 * n - 1 - p, p)
            sk = jnp.transpose(jnp.broadcast_to(seg_s[d, pl.ds(hi, 1), :], (HALF, HALF)))
            pos_k = p * HALF + lax.broadcasted_iota(jnp.int32, (HALF, HALF), 0)
            ok = (sk == sq) & (pos_k <= pos_q)
            b_s[t, h * HALF:(h + 1) * HALF, :] = jnp.where(ok, 0.0, -jnp.inf)
        return 0

    with jax.named_scope("mask"):
        seg_all().wait_recv()
        lax.fori_loop(0, n_l + n_h, mask_step, 0)
        diag(1)

    rows_g = g_sz * HALF
    scale = LOG2E * DH ** -0.5
    neg = -jnp.inf

    def fold(op, a):
        return op(a.reshape(a.shape[0] // 8, 8, HALF), axis=0)

    def across(op, a):
        return jnp.broadcast_to(op(a, axis=0, keepdims=True), a.shape)

    def heads(s, j):
        return s[:, j * HALF:(j + 1) * HALF]

    def probs(s, m):
        return jnp.exp2((s.reshape(s.shape[0] // 8, 8, HALF) - m[None]) * scale).reshape(s.shape)

    def low(g):
        q = q_s[1, g * g_sz:(g + 1) * g_sz].reshape(rows_g, DH)
        k = kv_s[g, 0:n, 0].reshape(n_l * KB, DH)
        s = lax.dot_general(k, q, (((1,), (1,)), ((), ())), preferred_element_type=F32)
        for j in range(g_sz):
            mx = None
            for t in range(n_l):
                sj = heads(s[t * KB:(t + 1) * KB], j) + b_s[t]
                s_s[t, j] = sj
                f = fold(jnp.max, sj)
                mx = f if mx is None else jnp.maximum(mx, f)
            ml_s[g, j] = across(jnp.max, mx)
        v = jnp.concatenate([kv_s[g, p, 1] for p in range(n)], axis=1)
        ps = []
        for j in range(g_sz):
            m = ml_s[g, j]
            m = jnp.where(m == neg, 0.0, m)
            cols, tot = [], None
            for t in range(n_l):
                p = probs(s_s[t, j], m)
                f = fold(jnp.sum, p)
                tot = f if tot is None else tot + f
                cols.append(p.astype(BF16))
            ll_s[g, j] = tot
            ps.append(jnp.concatenate(cols, axis=0))
        al_s[g] = jnp.dot(v, jnp.concatenate(ps, axis=1), preferred_element_type=F32)

    def rest(g):
        for j in range(g_sz):
            m_s[0, j] = jnp.full((8, HALF), neg, F32)
            m_s[1, j] = ml_s[g, j]
        with jax.named_scope(f"hscores#g={g}"):
            for t in range(n_h):
                ab, kb = mixed(t)
                q = q_s[ab, g * g_sz:(g + 1) * g_sz].reshape(rows_g, DH)
                k = kv_s[g, pl.ds(kb * 2, 2), 0].reshape(KB, DH)
                s = lax.dot_general(k, q, (((1,), (1,)), ((), ())), preferred_element_type=F32)
                for j in range(g_sz):
                    sj = heads(s, j) + b_s[n_l + t]
                    s_s[t, j] = sj
                    m_s[ab, j] = jnp.maximum(m_s[ab, j], fold(jnp.max, sj))
        for ab in range(2):
            for j in range(g_sz):
                m_s[ab, j] = across(jnp.max, m_s[ab, j])
        for j in range(g_sz):
            corr = jnp.exp2((ml_s[g, j] - m_s[1, j]) * scale)
            l_s[0, j] = jnp.zeros((8, HALF), F32)
            l_s[1, j] = ll_s[g, j] * corr
            a = heads(al_s[g], j)
            a_s[1, :, j * HALF:(j + 1) * HALF] = (a.reshape(DH // 8, 8, HALF) * corr[None]).reshape(DH, HALF)
        a_s[0] = jnp.zeros((DH, rows_g), F32)
        with jax.named_scope(f"hvalues#g={g}"):
            for t in range(n_h):
                ab, kb = mixed(t)
                v = jnp.concatenate([kv_s[g, kb * 2, 1], kv_s[g, kb * 2 + 1, 1]], axis=1)
                ps = []
                for j in range(g_sz):
                    p = probs(s_s[t, j], m_s[ab, j])
                    l_s[ab, j] += fold(jnp.sum, p)
                    ps.append(p.astype(BF16))
                a_s[ab] += jnp.dot(v, jnp.concatenate(ps, axis=1), preferred_element_type=F32)
        for ab in range(2):
            for j in range(g_sz):
                l = jnp.sum(l_s[ab, j], axis=0, keepdims=True)
                o = jnp.transpose(heads(a_s[ab], j) / l).astype(BF16)
                o_s[ab * HALF:(ab + 1) * HALF, (g * g_sz + j) * DH:(g * g_sz + j + 1) * DH] = o

    after_low = [
        [(forward, 3), (own, 6), (diag, 2)],
        [(forward, 4), (own, 7), (diag, 3)],
        [(forward, 5), (diag, 4)],
        [(forward, 6), (diag, 5)],
    ]
    after_rest = [[(forward, 7)], [(diag, 6)], [], []]
    for g in range(n_kv):
        hook(f"arrived_low#g={g}", (arrived, g))
        with jax.named_scope(f"low#g={g}"):
            low(g)
        hook(f"hook_low#g={g}", *after_low[g])

    for hf in range(2):
        for gg in range(2):
            g = hf * 2 + gg
            hook(f"arrived_high#g={g}", (arrived, n_kv + g))
            with jax.named_scope(f"rest#g={g}"):
                rest(g)
            hook(f"hook_rest#g={g}", *after_rest[g])
        if hf == 0:
            with jax.named_scope("wait_wo"):
                for j in range(n_q):
                    wait(2 + n_q + j)
        with jax.named_scope(f"wo#h={hf}"):
            for j in range(n_q):
                o = o_s[:, hf * half_k:(hf + 1) * half_k]
                y = jnp.dot(o, w_s[j, hf * half_k:(hf + 1) * half_k, :], preferred_element_type=F32)
                if hf == 0:
                    y_s[j] = y
                else:
                    y_ref[:, j * NC:(j + 1) * NC] = (y_s[j] + y).astype(BF16)
        if hf == 0:
            hook("hook_wo", (diag, 7))

    with jax.named_scope("tail"):
        seg_all().wait_send()
        ref = kv_s.at[:, pl.ds(0, 2 * (n - 1))]
        pltpu.make_async_remote_copy(
            src_ref=ref, dst_ref=ref, send_sem=send_sem, recv_sem=rs_sem.at[0],
            device_id={"cp": sib}, device_id_type=MESH).wait_send()


def solution(mesh):
    n = mesh.shape["cp"]

    def local(x, seg, wq, wk, wv, wo):
        lq, d = x.shape
        hq = wq.shape[1] // DH
        hkv = wk.shape[1] // DH
        g_sz = hq // hkv
        n_q = wq.shape[1] // NC
        dma = pltpu.SemaphoreType.DMA
        anyspec = pl.BlockSpec(memory_space=pl.ANY)
        return pl.pallas_call(
            functools.partial(_kernel, n, g_sz),
            out_shape=pltpu.VMEM((lq, wo.shape[1]), BF16),
            in_specs=[anyspec] * 6,
            out_specs=pl.BlockSpec(memory_space=pltpu.VMEM),
            scratch_shapes=[
                pltpu.VMEM((lq, d), BF16),
                pltpu.VMEM((n_q + 2, d, NC), BF16),
                pltpu.VMEM((hkv, 2 * n, 2, HALF, DH), BF16),
                pltpu.VMEM((2, hq, HALF, DH), BF16),
                pltpu.VMEM((lq, hq * DH), BF16),
                pltpu.VMEM((n // 2 + 1, g_sz, KB, HALF), F32),
                pltpu.VMEM((n + 1, KB, HALF), F32),
                pltpu.VMEM((2, g_sz, 8, HALF), F32),
                pltpu.VMEM((2, g_sz, 8, HALF), F32),
                pltpu.VMEM((2, DH, g_sz * HALF), F32),
                pltpu.VMEM((hkv, g_sz, 8, HALF), F32),
                pltpu.VMEM((hkv, g_sz, 8, HALF), F32),
                pltpu.VMEM((hkv, DH, g_sz * HALF), F32),
                pltpu.VMEM((n_q, lq, NC), F32),
                pltpu.VMEM((n, 2, HALF), jnp.int32),
                dma, dma((2 * n_q + 4,)), dma, dma,
                dma, dma((2 * hkv,)), dma((2 * hkv,)), dma((2 * hkv,)), dma,
            ],
            compiler_params=pltpu.CompilerParams(
                collective_id=0, has_side_effects=True, vmem_limit_bytes=60 * 2 ** 20),
            name="layer",
        )(x, seg.reshape(2, HALF), wq, wk, wv, wo)

    rows = P(("dp", "cp"), None)
    return jax.shard_map(local, mesh=mesh, in_specs=(rows, P(("dp", "cp")), P(), P(), P(), P()), out_specs=rows, check_vma=False)
```

time: 49.7 us -> 45.3 us (0.911)
  Pallas kernels: 46.8 us -> 44 us
  local copies, waits for them, and re-layouts: 2.85 us -> 1.23 us
    pallas_call x1, Pallas kernels: 46.8 us -> 44 us  [local(): pl.pallas_call(functools.partial(_kernel, n, g_sz), out_shape=pltpu.VMEM(...]
    unnamed x1, local copies, waits for them, and re-layouts: 2.85 us -> 1.23 us
where the time goes in v2:
time: 45.3 us; the launch traced here: 45.2 us
  Pallas kernels  44 us (97%)
  local copies, waits for them, and re-layouts  1.23 us (3%)
    pallas_call x1, Pallas kernels, local(): pl.pallas_call(functools.partial(_kernel, n, g_sz), out_shape=pltpu.VMEM(...  44 us
    unnamed x1, local copies, waits for them, and re-layouts  1.23 us

profile of v2, /device:TPU:0, one launch (start us, length us, event | category | flops | bytes accessed | tf_op | source)
XLA Modules:
  0.0 45.2 jit_solution(10111306985301606151)
XLA Ops:
  0.0 44.0 %layer.1 = bf16[256,3584]{1,0:T(8,128)(2,1)S(1)} custom-call(bf16[256,3584]{1,0:T(8,128)(2,1)} %x_hbm.1, s32[2,128]{1,0:T(2,128)} %bitcast.1, bf16[3584,3584]{1,0:T(8,128)(2,1)} %wq_hbm.1, bf16[3584,512]{1,0:T(8,128)(2,1)} %wk_hbm.1, bf16[3584,512]{1,0:T(8,128)(2,1)} %wv_hbm.1, bf16[3584,3584]{1,0:T(8,128)(2,1)} %wo_hbm.1), custom_call_target="tpu_custom_call" | custom-call | tf_op jit(solution)/shard_map/layer/pallas_call | solution.py:338
  44.0 1.2 %copy.8 = bf16[256,3584]{1,0:T(8,128)(2,1)} copy(bf16[256,3584]{1,0:T(8,128)(2,1)S(1)} %layer.1) | data formatting | bytes 3670016

commit v3 on v2

v3 whole, which is shorter than its diff:
```python
import functools

import jax
import jax.numpy as jnp
from jax import lax
from jax.experimental import pallas as pl
from jax.experimental.pallas import tpu as pltpu
from jax.sharding import PartitionSpec as P

DH = 128
HALF = 128
KB = 256
NC = 512
MESH = pl.DeviceIdType.MESH
F32 = jnp.float32
BF16 = jnp.bfloat16
LOG2E = 1.4426950408889634


def _kernel(n, g_sz, x_hbm, seg_hbm, wq_hbm, wk_hbm, wv_hbm, wo_hbm, y_ref,
            x_s, w_s, kv_s, q_s, o_s, s_s, b_s, m_s, l_s, a_s, ml_s, ll_s, al_s, y_s, seg_s,
            x_sem, w_sem, ss_sem, sr_sem, send_sem, rn_sem, rd_sem, rs_sem, loc_sem):
    me = lax.axis_index("cp")
    c, xx, yy = me % 2, (me // 2) % 2, me // 4

    def dev(dy, dx, dc):
        ny = 1 - yy if dy else yy
        nx = 1 - xx if dx else xx
        nc = 1 - c if dc else c
        return ny * 4 + nx * 2 + nc

    d_model = x_s.shape[1]
    n_q = wq_hbm.shape[1] // NC
    n_kv = wk_hbm.shape[1] // DH
    half_k = d_model // 2
    peers = [dev(k // 4, (k // 2) % 2, k % 2) for k in range(n)]
    sib = peers[1]

    def load(i):
        if i < n_kv:
            cols = pl.ds(i * DH, DH)
            slot, lo = i // 2, (i % 2) * 2 * DH
            return [
                pltpu.make_async_copy(wk_hbm.at[:, cols], w_s.at[slot, :, pl.ds(lo, DH)], w_sem.at[i]),
                pltpu.make_async_copy(wv_hbm.at[:, cols], w_s.at[slot, :, pl.ds(lo + DH, DH)], w_sem.at[n_kv + 2 * n_q + i]),
            ]
        j = i - n_kv
        if j < n_q:
            return [pltpu.make_async_copy(wq_hbm.at[:, pl.ds(j * NC, NC)], w_s.at[2 + j], w_sem.at[i])]
        j = j - n_q
        return [pltpu.make_async_copy(wo_hbm.at[:, pl.ds(j * NC, NC)], w_s.at[j], w_sem.at[i])]

    def start(i):
        for cp in load(i):
            cp.start()

    def wait(i):
        for cp in load(i):
            cp.wait()

    x_cp = pltpu.make_async_copy(x_hbm, x_s, x_sem)
    seg_cp = pltpu.make_async_copy(seg_hbm, seg_s.at[me], loc_sem)
    x_cp.start()
    start(0)
    seg_cp.start()

    def seg_copy(k):
        return pltpu.make_async_remote_copy(
            src_ref=seg_s.at[me], dst_ref=seg_s.at[me], send_sem=ss_sem, recv_sem=sr_sem,
            device_id={"cp": peers[k]}, device_id_type=MESH)

    def seg_all():
        ref = seg_s.at[pl.ds(0, n - 1)]
        return pltpu.make_async_remote_copy(
            src_ref=ref, dst_ref=ref, send_sem=ss_sem, recv_sem=sr_sem,
            device_id={"cp": sib}, device_id_type=MESH)

    barrier = pltpu.get_barrier_semaphore()
    for k in range(1, n):
        pl.semaphore_signal(barrier, inc=1, device_id={"cp": peers[k]}, device_id_type=MESH)

    xn, yn, dg = peers[2], peers[4], peers[6]
    first, second = xn * (1 - c) + yn * c, yn * (1 - c) + xn * c

    units = [(ab, 2 * hf + gg) for hf in range(n_kv // 2) for ab in range(2) for gg in range(2)]

    def chunk(u, src_dev, to, recv):
        ab, g = units[u]
        ref = kv_s.at[g, src_dev if ab == 0 else 2 * n - 1 - src_dev]
        return pltpu.make_async_remote_copy(
            src_ref=ref, dst_ref=ref, send_sem=send_sem, recv_sem=recv.at[u],
            device_id={"cp": to}, device_id_type=MESH)

    def wait_chunks(u, count, recv):
        ref = kv_s.at[u % n_kv, pl.ds(0, count)]
        pltpu.make_async_remote_copy(
            src_ref=ref, dst_ref=ref, send_sem=send_sem, recv_sem=recv.at[u],
            device_id={"cp": sib}, device_id_type=MESH).wait_recv()

    def own(u):
        chunk(u, me, xn, rn_sem).start()
        chunk(u, me, yn, rn_sem).start()
        chunk(u, me, sib, rs_sem).start()

    def forward(u):
        wait_chunks(u, 2, rn_sem)
        chunk(u, first, second, rd_sem).start()
        chunk(u, xn, sib, rs_sem).start()
        chunk(u, yn, sib, rs_sem).start()

    def diag(u):
        wait_chunks(u, 1, rd_sem)
        chunk(u, dg, sib, rs_sem).start()

    def arrived(u):
        wait_chunks(u, 4, rs_sem)

    f, d, o = forward, diag, own
    table = {
        "q0": ([], [(f, 0), (o, 3)]),
        "q2": ([], [(f, 1)]),
        "q3": ([(f, 0), (o, 3)], [(f, 2), (o, 4), (d, 0)]),
        "q4": ([(f, 1)], [(f, 3), (o, 5)]),
        "q5": ([(f, 2), (o, 4)], [(d, 1)]),
        "q6": ([(d, 0)], [(d, 2)]),
        "mask": ([(f, 3), (o, 5), (d, 1)], [(f, 4), (o, 6)]),
        "s0": ([(d, 2)], [(d, 3)]),
        "s1": ([(f, 4), (o, 6), (d, 3)], [(f, 5), (o, 7)]),
        "s2": ([], [(d, 4)]),
        "s3": ([(f, 5), (o, 7), (d, 4)], [(f, 6), (d, 5)]),
        "s4": ([(f, 6), (d, 5)], [(f, 7)]),
        "wo0": ([(f, 7), (d, 6)], [(d, 6), (d, 7)]),
        "s5": ([(d, 7)], []),
    }

    def slot(name):
        early, late = table.get(name, ([], []))
        for cond, acts in ((me < 2, early), (me >= 2, late)):
            if acts:
                @pl.when(cond)
                def _():
                    with jax.named_scope(f"slot_{name}"):
                        for act, u in acts:
                            act(u)

    with jax.named_scope("wait_x"):
        x_cp.wait()
        start(1)
    for g in range(n_kv):
        with jax.named_scope(f"wait_kv#g={g}"):
            wait(g)
            if g == 0:
                start(2)
                start(3)
            else:
                start(n_kv + g - 1)
        with jax.named_scope(f"kv#g={g}"):
            lo = (g % 2) * 2 * DH
            r = sum(jnp.dot(x_s[:, h * half_k:(h + 1) * half_k], w_s[g // 2, h * half_k:(h + 1) * half_k, lo:lo + 2 * DH],
                            preferred_element_type=F32) for h in range(2))
            for ab in range(2):
                piece = me if ab == 0 else 2 * n - 1 - me
                part = r[ab * HALF:(ab + 1) * HALF]
                kv_s[g, piece, 0] = part[:, :DH].astype(BF16)
                kv_s[g, piece, 1] = jnp.transpose(part[:, DH:]).astype(BF16)
        for cond, acts in ((me >= 2, {0: [0], 1: [1, 2]}), (me < 2, {2: [0, 1, 2]})):
            if g in acts:
                @pl.when(cond)
                def _():
                    if acts[g][0] == 0:
                        with jax.named_scope("barrier"):
                            pl.semaphore_wait(barrier, n - 1)
                    for u in acts[g]:
                        own(u)
                    if acts[g][0] == 0:
                        seg_cp.wait()
                        for k in range(1, n):
                            seg_copy(k).start()

    def q_chunk(j):
        r = jnp.dot(x_s[...], w_s[2 + j], preferred_element_type=F32).astype(BF16)
        for hh in range(NC // DH):
            for ab in range(2):
                q_s[ab, j * (NC // DH) + hh] = r[ab * HALF:(ab + 1) * HALF, hh * DH:(hh + 1) * DH]

    for j in range(n_q):
        with jax.named_scope(f"wait_q#j={j}"):
            wait(n_kv + j)
            start(n_kv + j + 3)
        with jax.named_scope(f"q#j={j}"):
            q_chunk(j)
        slot(f"q{j}")
    for j in range(n_kv + n_q + 3, n_kv + 2 * n_q):
        start(j)

    n_l = n // 2
    n_h = n_l + 1
    n_a = me // 2 + 1

    def mixed(t):
        ab = jnp.where(t >= n_a, 1, 0)
        return ab, t + ab * (n_l - n_a)

    def mask_step(t, _):
        ab, kb = mixed(t - n_l)
        ab = jnp.where(t < n_l, 1, ab)
        kb = jnp.where(t < n_l, t, kb)
        qp = jnp.where(ab == 1, 2 * n - 1 - me, me)
        sq = seg_s[me, pl.ds(ab, 1), :]
        pos_q = qp * HALF + lax.broadcasted_iota(jnp.int32, (HALF, HALF), 1)
        for h in range(2):
            p = kb * 2 + h
            hi = jnp.where(p >= n, 1, 0)
            d = jnp.where(p >= n, 2 * n - 1 - p, p)
            sk = jnp.transpose(jnp.broadcast_to(seg_s[d, pl.ds(hi, 1), :], (HALF, HALF)))
            pos_k = p * HALF + lax.broadcasted_iota(jnp.int32, (HALF, HALF), 0)
            ok = (sk == sq) & (pos_k <= pos_q)
            b_s[t, h * HALF:(h + 1) * HALF, :] = jnp.where(ok, 0.0, -jnp.inf)
        return 0

    with jax.named_scope("mask"):
        seg_all().wait_recv()
        lax.fori_loop(0, n_l + n_h, mask_step, 0)
    slot("mask")

    rows_g = g_sz * HALF
    scale = LOG2E * DH ** -0.5
    neg = -jnp.inf

    def fold(op, a):
        return op(a.reshape(a.shape[0] // 8, 8, HALF), axis=0)

    def across(op, a):
        return jnp.broadcast_to(op(a, axis=0, keepdims=True), a.shape)

    def heads(s, j):
        return s[:, j * HALF:(j + 1) * HALF]

    def probs(s, m):
        return jnp.exp2((s.reshape(s.shape[0] // 8, 8, HALF) - m[None]) * scale).reshape(s.shape)

    tiles = [range(lo, min(lo + 2, g_sz)) for lo in range(0, g_sz, 2)]

    def span(js):
        return slice(js[0] * HALF, (js[-1] + 1) * HALF)

    def q_of(ab, g, js):
        return q_s[ab, g * g_sz + js[0]:g * g_sz + js[-1] + 1].reshape(len(js) * HALF, DH)

    def scores_low(i, g, js):
        k = kv_s[g, 0:n, 0].reshape(n_l * KB, DH)
        s = lax.dot_general(k, q_of(1, g, js), (((1,), (1,)), ((), ())), preferred_element_type=F32)
        for jj, j in enumerate(js):
            mx = None
            for t in range(n_l):
                sj = heads(s[t * KB:(t + 1) * KB], jj) + b_s[t]
                s_s[i % 2, t, j] = sj
                f = fold(jnp.max, sj)
                mx = f if mx is None else jnp.maximum(mx, f)
            ml_s[g, j] = across(jnp.max, mx)

    def values_low(i, g, js):
        v = jnp.concatenate([kv_s[g, p, 1] for p in range(n)], axis=1)
        ps = []
        for j in js:
            m = ml_s[g, j]
            m = jnp.where(m == neg, 0.0, m)
            cols, tot = [], None
            for t in range(n_l):
                p = probs(s_s[i % 2, t, j], m)
                f = fold(jnp.sum, p)
                tot = f if tot is None else tot + f
                cols.append(p.astype(BF16))
            ll_s[g, j] = tot
            ps.append(jnp.concatenate(cols, axis=0))
        al_s[g, :, span(js)] = jnp.dot(v, jnp.concatenate(ps, axis=1), preferred_element_type=F32)

    order = [0, n_h - 1] + list(range(1, n_h - 1))
    every = range(g_sz)

    def scores_rest(i, g, t):
        ab, kb = (0, 0) if t == 0 else (1, n - 1 - me // 2) if t == n_h - 1 else mixed(t)
        k = kv_s[g, pl.ds(kb * 2, 2), 0].reshape(KB, DH)
        s = lax.dot_general(k, q_of(ab, g, every), (((1,), (1,)), ((), ())), preferred_element_type=F32)
        for j in every:
            sj = heads(s, j) + b_s[n_l + t]
            s_s[i % 2, t, j] = sj
            mx = fold(jnp.max, sj)
            if t == n_h - 1:
                mx = jnp.maximum(mx, ml_s[g, j])
            elif t > 0:
                mx = jnp.maximum(mx, m_s[g % 2, ab, j])
            m_s[g % 2, ab, j] = mx

    def scores_end(i, g):
        for ab in range(2):
            for j in every:
                m_s[g % 2, ab, j] = across(jnp.max, m_s[g % 2, ab, j])

    def values_rest(i, g, t):
        ab, kb = (0, 0) if t == 0 else (1, n - 1 - me // 2) if t == n_h - 1 else mixed(t)
        v = jnp.concatenate([kv_s[g, kb * 2, 1], kv_s[g, kb * 2 + 1, 1]], axis=1)
        ps, corrs = [], []
        for j in every:
            p = probs(s_s[i % 2, t, j], m_s[g % 2, ab, j])
            l = fold(jnp.sum, p)
            if t == n_h - 1:
                corrs.append(jnp.exp2((ml_s[g, j] - m_s[g % 2, 1, j]) * scale))
                l += ll_s[g, j] * corrs[-1]
            elif t > 0:
                l += l_s[ab, j]
            l_s[ab, j] = l
            ps.append(p.astype(BF16))
        a = jnp.dot(v, jnp.concatenate(ps, axis=1), preferred_element_type=F32)
        if t == n_h - 1:
            old = [(al_s[g, :, span([j])].reshape(DH // 8, 8, HALF) * corrs[j][None]).reshape(DH, HALF) for j in every]
            a += jnp.concatenate(old, axis=1)
        elif t > 0:
            a += a_s[ab]
        a_s[ab] = a

    def values_end(i, g):
        for ab in range(2):
            for j in every:
                r = 1.0 / jnp.sum(l_s[ab, j], axis=0, keepdims=True)
                o = jnp.transpose(a_s[ab, :, span([j])] * r).astype(BF16)
                o_s[ab * HALF:(ab + 1) * HALF, (g * g_sz + j) * DH:(g * g_sz + j + 1) * DH] = o

    def parts(i, low, rest, end):
        if i is None:
            return []
        ab, g = units[i]
        if ab == 0:
            return [functools.partial(low, i, g, js) for js in tiles]
        done = [functools.partial(end, i, g)]
        return [functools.partial(rest, i, g, t) for t in order] + done

    def block(i, j):
        if i is not None:
            with jax.named_scope(f"arrived#i={i}"):
                arrived(i)
        with jax.named_scope(f"block#s={i}#v={j}"):
            a = parts(i, scores_low, scores_rest, scores_end)
            b = parts(j, values_low, values_rest, values_end)
            for k in range(max(len(a), len(b))):
                for lst in (a, b):
                    if k < len(lst):
                        lst[k]()

    def project(hf):
        if hf == 0:
            with jax.named_scope("wait_wo"):
                for j in range(n_q):
                    wait(n_kv + n_q + j)
        with jax.named_scope(f"wo#h={hf}"):
            for j in range(n_q):
                o = o_s[:, hf * half_k:(hf + 1) * half_k]
                y = jnp.dot(o, w_s[j, hf * half_k:(hf + 1) * half_k, :], preferred_element_type=F32)
                if hf == 0:
                    y_s[j] = y
                else:
                    y_ref[:, j * NC:(j + 1) * NC] = (y_s[j] + y).astype(BF16)

    last = len(units) - 1
    block(0, None)
    slot("s0")
    for i in range(1, last + 1):
        block(i, i - 1)
        slot(f"s{i}")
        if i == n_kv:
            project(0)
            slot("wo0")
    block(None, last)
    project(1)

    with jax.named_scope("tail"):
        seg_all().wait_send()
        ref = kv_s.at[:, pl.ds(0, 2 * (n - 1))]
        pltpu.make_async_remote_copy(
            src_ref=ref, dst_ref=ref, send_sem=send_sem, recv_sem=rs_sem.at[0],
            device_id={"cp": sib}, device_id_type=MESH).wait_send()


def solution(mesh):
    n = mesh.shape["cp"]

    def local(x, seg, wq, wk, wv, wo):
        lq, d = x.shape
        hq = wq.shape[1] // DH
        hkv = wk.shape[1] // DH
        g_sz = hq // hkv
        n_q = wq.shape[1] // NC
        dma = pltpu.SemaphoreType.DMA
        anyspec = pl.BlockSpec(memory_space=pl.ANY)
        return pl.pallas_call(
            functools.partial(_kernel, n, g_sz),
            out_shape=pltpu.VMEM((lq, wo.shape[1]), BF16),
            in_specs=[anyspec] * 6,
            out_specs=pl.BlockSpec(memory_space=pltpu.VMEM),
            scratch_shapes=[
                pltpu.VMEM((lq, d), BF16),
                pltpu.VMEM((n_q + 2, d, NC), BF16),
                pltpu.VMEM((hkv, 2 * n, 2, HALF, DH), BF16),
                pltpu.VMEM((2, hq, HALF, DH), BF16),
                pltpu.VMEM((lq, hq * DH), BF16),
                pltpu.VMEM((2, n // 2 + 1, g_sz, KB, HALF), F32),
                pltpu.VMEM((n + 1, KB, HALF), F32),
                pltpu.VMEM((2, 2, g_sz, 8, HALF), F32),
                pltpu.VMEM((2, g_sz, 8, HALF), F32),
                pltpu.VMEM((2, DH, g_sz * HALF), F32),
                pltpu.VMEM((hkv, g_sz, 8, HALF), F32),
                pltpu.VMEM((hkv, g_sz, 8, HALF), F32),
                pltpu.VMEM((hkv, DH, g_sz * HALF), F32),
                pltpu.VMEM((n_q, lq, NC), F32),
                pltpu.VMEM((n, 2, HALF), jnp.int32),
                dma, dma((2 * n_q + 2 * hkv,)), dma, dma,
                dma, dma((2 * hkv,)), dma((2 * hkv,)), dma((2 * hkv,)), dma,
            ],
            compiler_params=pltpu.CompilerParams(
                collective_id=0, has_side_effects=True, vmem_limit_bytes=60 * 2 ** 20),
            name="layer",
        )(x, seg.reshape(2, HALF), wq, wk, wv, wo)

    rows = P(("dp", "cp"), None)
    return jax.shard_map(local, mesh=mesh, in_specs=(rows, P(("dp", "cp")), P(), P(), P(), P()), out_specs=rows, check_vma=False)
```

time: 45.3 us -> 40.1 us (0.89)
  Pallas kernels: 44 us -> 38.5 us
    pallas_call x1, Pallas kernels: 44 us -> 38.5 us  [local(): pl.pallas_call(functools.partial(_kernel, n, g_sz), out_shape=pltpu.VMEM(...]
where the time goes in v3:
time: 40.1 us; the launch traced here: 39.8 us
  Pallas kernels  38.5 us (96%)
  local copies, waits for them, and re-layouts  1.23 us (3%)
    pallas_call x1, Pallas kernels, local(): pl.pallas_call(functools.partial(_kernel, n, g_sz), out_shape=pltpu.VMEM(...  38.5 us
    unnamed x1, local copies, waits for them, and re-layouts  1.23 us

profile of v3, /device:TPU:0, one launch (start us, length us, event | category | flops | bytes accessed | tf_op | source)
XLA Modules:
  0.0 39.8 jit_solution(8983484545154141514)
XLA Ops:
  0.0 38.5 %layer.1 = bf16[256,3584]{1,0:T(8,128)(2,1)S(1)} custom-call(bf16[256,3584]{1,0:T(8,128)(2,1)} %x_hbm.1, s32[2,128]{1,0:T(2,128)} %bitcast.1, bf16[3584,3584]{1,0:T(8,128)(2,1)} %wq_hbm.1, bf16[3584,512]{1,0:T(8,128)(2,1)} %wk_hbm.1, bf16[3584,512]{1,0:T(8,128)(2,1)} %wv_hbm.1, bf16[3584,3584]{1,0:T(8,128)(2,1)} %wo_hbm.1), custom_call_target="tpu_custom_call" | custom-call | tf_op jit(solution)/shard_map/layer/pallas_call | solution.py:395
  38.5 1.2 %copy.8 = bf16[256,3584]{1,0:T(8,128)(2,1)} copy(bf16[256,3584]{1,0:T(8,128)(2,1)S(1)} %layer.1) | data formatting | bytes 3670016

commit v4 on v3

--- a/solution.py
+++ b/solution.py
@@ -18,7 +18,7 @@
 
 
 def _kernel(n, g_sz, x_hbm, seg_hbm, wq_hbm, wk_hbm, wv_hbm, wo_hbm, y_ref,
-            x_s, w_s, kv_s, q_s, o_s, s_s, b_s, m_s, l_s, a_s, ml_s, ll_s, al_s, y_s, seg_s,
+            x_s, w_s, kv_s, q_s, s_s, b_s, m_s, l_s, a_s, ml_s, ll_s, al_s, y_s, seg_s,
             x_sem, w_sem, ss_sem, sr_sem, send_sem, rn_sem, rd_sem, rs_sem, loc_sem):
     me = lax.axis_index("cp")
     c, xx, yy = me % 2, (me // 2) % 2, me // 4
@@ -37,18 +37,18 @@
     sib = peers[1]
 
     def load(i):
-        if i < n_kv:
-            cols = pl.ds(i * DH, DH)
-            slot, lo = i // 2, (i % 2) * 2 * DH
+        if i < 3:
+            slot, rows = (0, pl.ds(i * half_k, half_k)) if i < 2 else (1, pl.ds(0, d_model))
+            cols = pl.ds(slot * 2 * DH, 2 * DH)
             return [
-                pltpu.make_async_copy(wk_hbm.at[:, cols], w_s.at[slot, :, pl.ds(lo, DH)], w_sem.at[i]),
-                pltpu.make_async_copy(wv_hbm.at[:, cols], w_s.at[slot, :, pl.ds(lo + DH, DH)], w_sem.at[n_kv + 2 * n_q + i]),
+                pltpu.make_async_copy(w.at[rows, cols], w_s.at[slot, rows, pl.ds(t * 2 * DH, 2 * DH)], w_sem.at[i + t * 3])
+                for t, w in enumerate((wk_hbm, wv_hbm))
             ]
-        j = i - n_kv
-        if j < n_q:
-            return [pltpu.make_async_copy(wq_hbm.at[:, pl.ds(j * NC, NC)], w_s.at[2 + j], w_sem.at[i])]
-        j = j - n_q
-        return [pltpu.make_async_copy(wo_hbm.at[:, pl.ds(j * NC, NC)], w_s.at[j], w_sem.at[i])]
+        if i < 3 + n_q:
+            j = i - 3
+            return [pltpu.make_async_copy(wq_hbm.at[:, pl.ds(j * NC, NC)], w_s.at[2 + j], w_sem.at[i + 3])]
+        j = i - 3 - n_q
+        return [pltpu.make_async_copy(wo_hbm.at[:, pl.ds(j * NC, NC)], w_s.at[j], w_sem.at[i + 3])]
 
     def start(i):
         for cp in load(i):
@@ -58,10 +58,15 @@
         for cp in load(i):
             cp.wait()
 
-    x_cp = pltpu.make_async_copy(x_hbm, x_s, x_sem)
+    def x_copy(h):
+        cols = pl.ds(h * half_k, half_k)
+        return pltpu.make_async_copy(x_hbm.at[:, cols], x_s.at[:, cols], x_sem.at[h])
+
     seg_cp = pltpu.make_async_copy(seg_hbm, seg_s.at[me], loc_sem)
-    x_cp.start()
+    x_copy(0).start()
     start(0)
+    x_copy(1).start()
+    start(1)
     seg_cp.start()
 
     def seg_copy(k):
@@ -82,7 +87,7 @@
     xn, yn, dg = peers[2], peers[4], peers[6]
     first, second = xn * (1 - c) + yn * c, yn * (1 - c) + xn * c
 
-    units = [(ab, 2 * hf + gg) for hf in range(n_kv // 2) for ab in range(2) for gg in range(2)]
+    units = [(ab, g) for g in range(n_kv) for ab in range(2)]
 
     def chunk(u, src_dev, to, recv):
         ab, g = units[u]
@@ -117,81 +122,75 @@
 
     f, d, o = forward, diag, own
     table = {
-        "q0": ([], [(f, 0), (o, 3)]),
-        "q2": ([], [(f, 1)]),
-        "q3": ([(f, 0), (o, 3)], [(f, 2), (o, 4), (d, 0)]),
-        "q4": ([(f, 1)], [(f, 3), (o, 5)]),
-        "q5": ([(f, 2), (o, 4)], [(d, 1)]),
-        "q6": ([(d, 0)], [(d, 2)]),
-        "mask": ([(f, 3), (o, 5), (d, 1)], [(f, 4), (o, 6)]),
-        "s0": ([(d, 2)], [(d, 3)]),
-        "s1": ([(f, 4), (o, 6), (d, 3)], [(f, 5), (o, 7)]),
-        "s2": ([], [(d, 4)]),
-        "s3": ([(f, 5), (o, 7), (d, 4)], [(f, 6), (d, 5)]),
-        "s4": ([(f, 6), (d, 5)], [(f, 7)]),
-        "wo0": ([(f, 7), (d, 6)], [(d, 6), (d, 7)]),
-        "s5": ([(d, 7)], []),
+        "kv1": ([], [(o, 1)]),
+        "q0": ([], [(f, 0), (o, 2)]),
+        "q1": ([(o, 1)], []),
+        "q2": ([], [(f, 1), (o, 3)]),
+        "q3": ([(f, 0), (o, 2)], [(d, 0)]),
+        "q4": ([(f, 1)], [(f, 2), (o, 4)]),
+        "q5": ([(o, 3), (d, 0)], [(d, 1)]),
+        "q6": ([(f, 2), (o, 4)], [(f, 3), (o, 5)]),
+        "s0": ([(o, 5), (d, 1)], [(d, 2)]),
+        "s1": ([(f, 3), (o, 6), (d, 2)], [(f, 4)]),
+        "s2": ([(f, 4), (o, 7), (d, 3)], [(f, 5), (d, 3), (o, 6)]),
+        "w0": ([(f, 5), (d, 4)], [(d, 4), (o, 7)]),
+        "s3": ([], [(f, 6)]),
+        "s4": ([(f, 6), (d, 5)], [(d, 5), (f, 7)]),
+        "w1": ([(f, 7), (d, 6)], [(d, 6)]),
+        "s6": ([(d, 7)], [(d, 7)]),
     }
 
     def slot(name):
         early, late = table.get(name, ([], []))
+        def run(acts):
+            with jax.named_scope(f"slot_{name}"):
+                for act, u in acts:
+                    act(u)
+
+        if early == late:
+            return run(early)
         for cond, acts in ((me < 2, early), (me >= 2, late)):
             if acts:
-                @pl.when(cond)
-                def _():
-                    with jax.named_scope(f"slot_{name}"):
-                        for act, u in acts:
-                            act(u)
-
-    with jax.named_scope("wait_x"):
-        x_cp.wait()
-        start(1)
-    for g in range(n_kv):
-        with jax.named_scope(f"wait_kv#g={g}"):
-            wait(g)
-            if g == 0:
-                start(2)
-                start(3)
-            else:
-                start(n_kv + g - 1)
-        with jax.named_scope(f"kv#g={g}"):
-            lo = (g % 2) * 2 * DH
-            r = sum(jnp.dot(x_s[:, h * half_k:(h + 1) * half_k], w_s[g // 2, h * half_k:(h + 1) * half_k, lo:lo + 2 * DH],
-                            preferred_element_type=F32) for h in range(2))
+                pl.when(cond)(functools.partial(run, acts))
+
+    def begin(us):
+        with jax.named_scope("barrier"):
+            pl.semaphore_wait(barrier, n - 1)
+        seg_cp.wait()
+        for k in range(1, n):
+            seg_copy(k).start()
+        for u in us:
+            own(u)
+
+    def keep_kv(i, r):
+        for gg in range(2):
             for ab in range(2):
                 piece = me if ab == 0 else 2 * n - 1 - me
                 part = r[ab * HALF:(ab + 1) * HALF]
-                kv_s[g, piece, 0] = part[:, :DH].astype(BF16)
-                kv_s[g, piece, 1] = jnp.transpose(part[:, DH:]).astype(BF16)
-        for cond, acts in ((me >= 2, {0: [0], 1: [1, 2]}), (me < 2, {2: [0, 1, 2]})):
-            if g in acts:
-                @pl.when(cond)
-                def _():
-                    if acts[g][0] == 0:
-                        with jax.named_scope("barrier"):
-                            pl.semaphore_wait(barrier, n - 1)
-                    for u in acts[g]:
-                        own(u)
-                    if acts[g][0] == 0:
-                        seg_cp.wait()
-                        for k in range(1, n):
-                            seg_copy(k).start()
-
-    def q_chunk(j):
-        r = jnp.dot(x_s[...], w_s[2 + j], preferred_element_type=F32).astype(BF16)
-        for hh in range(NC // DH):
-            for ab in range(2):
-                q_s[ab, j * (NC // DH) + hh] = r[ab * HALF:(ab + 1) * HALF, hh * DH:(hh + 1) * DH]
-
-    for j in range(n_q):
-        with jax.named_scope(f"wait_q#j={j}"):
-            wait(n_kv + j)
-            start(n_kv + j + 3)
-        with jax.named_scope(f"q#j={j}"):
-            q_chunk(j)
-        slot(f"q{j}")
-    for j in range(n_kv + n_q + 3, n_kv + 2 * n_q):
-        start(j)
+                kv_s[2 * i + gg, piece, 0] = part[:, gg * DH:(gg + 1) * DH].astype(BF16)
+                kv_s[2 * i + gg, piece, 1] = jnp.transpose(part[:, (2 + gg) * DH:(3 + gg) * DH]).astype(BF16)
+
+    with jax.named_scope("wait_x0"):
+        x_copy(0).wait()
+        wait(0)
+        start(2)
+    with jax.named_scope("kv0a"):
+        y_s[0] = jnp.dot(x_s[:, :half_k], w_s[0, :half_k], preferred_element_type=F32)
+    with jax.named_scope("wait_x1"):
+        x_copy(1).wait()
+        wait(1)
+        start(3)
+    with jax.named_scope("kv0b"):
+        keep_kv(0, y_s[0] + jnp.dot(x_s[:, half_k:], w_s[0, half_k:], preferred_element_type=F32))
+    pl.when(me >= 2)(functools.partial(begin, [0]))
+    with jax.named_scope("wait_kv1"):
+        wait(2)
+        start(4)
+        start(5)
+    with jax.named_scope("kv1"):
+        keep_kv(1, jnp.dot(x_s[...], w_s[1], preferred_element_type=F32))
+    pl.when(me < 2)(functools.partial(begin, [0]))
+    slot("kv1")
 
     n_l = n // 2
     n_h = n_l + 1
@@ -201,7 +200,7 @@
         ab = jnp.where(t >= n_a, 1, 0)
         return ab, t + ab * (n_l - n_a)
 
-    def mask_step(t, _):
+    def mask_step(t):
         ab, kb = mixed(t - n_l)
         ab = jnp.where(t < n_l, 1, ab)
         kb = jnp.where(t < n_l, t, kb)
@@ -216,13 +215,32 @@
             pos_k = p * HALF + lax.broadcasted_iota(jnp.int32, (HALF, HALF), 0)
             ok = (sk == sq) & (pos_k <= pos_q)
             b_s[t, h * HALF:(h + 1) * HALF, :] = jnp.where(ok, 0.0, -jnp.inf)
-        return 0
-
-    with jax.named_scope("mask"):
-        seg_all().wait_recv()
-        lax.fori_loop(0, n_l + n_h, mask_step, 0)
-    slot("mask")
-
+
+    def q_chunk(j):
+        r = jnp.dot(x_s[...], w_s[2 + j], preferred_element_type=F32).astype(BF16)
+        for hh in range(NC // DH):
+            for ab in range(2):
+                q_s[ab, j * (NC // DH) + hh] = r[ab * HALF:(ab + 1) * HALF, hh * DH:(hh + 1) * DH]
+
+    nexts = [[6 + j] for j in range(n_q - 2)] + [[4 + n_q, 5 + n_q], [6 + n_q, 7 + n_q]]
+    for j in range(n_q):
+        with jax.named_scope(f"wait_q#j={j}"):
+            wait(3 + j)
+            for i in nexts[j]:
+                start(i)
+            if j == n_q - 2:
+                seg_all().wait_recv()
+        with jax.named_scope(f"q#j={j}"):
+            if j >= n_q - 2:
+                for t in range(n_l + n_h):
+                    if (t < n_l) == (j == n_q - 2):
+                        mask_step(t)
+            q_chunk(j)
+        slot(f"q{j}")
+    for i in range(8 + n_q, 3 + 2 * n_q):
+        start(i)
+
+    o_s = x_s
     rows_g = g_sz * HALF
     scale = LOG2E * DH ** -0.5
     neg = -jnp.inf
@@ -347,31 +365,34 @@
                     if k < len(lst):
                         lst[k]()
 
-    def project(hf):
-        if hf == 0:
+    cuts = [min(g * g_sz * DH // KB * KB, d_model) for g in range(n_kv)] + [d_model]
+
+    def project(g):
+        if g == 0:
             with jax.named_scope("wait_wo"):
                 for j in range(n_q):
-                    wait(n_kv + n_q + j)
-        with jax.named_scope(f"wo#h={hf}"):
+                    wait(3 + n_q + j)
+        rows = slice(cuts[g], cuts[g + 1])
+        with jax.named_scope(f"wo#g={g}"):
             for j in range(n_q):
-                o = o_s[:, hf * half_k:(hf + 1) * half_k]
-                y = jnp.dot(o, w_s[j, hf * half_k:(hf + 1) * half_k, :], preferred_element_type=F32)
-                if hf == 0:
+                y = jnp.dot(o_s[:, rows], w_s[j, rows, :], preferred_element_type=F32)
+                if g > 0:
+                    y += y_s[j]
+                if g < n_kv - 1:
                     y_s[j] = y
                 else:
-                    y_ref[:, j * NC:(j + 1) * NC] = (y_s[j] + y).astype(BF16)
-
-    last = len(units) - 1
+                    y_ref[:, j * NC:(j + 1) * NC] = y.astype(BF16)
+
     block(0, None)
     slot("s0")
-    for i in range(1, last + 1):
+    for i in range(1, len(units)):
         block(i, i - 1)
         slot(f"s{i}")
-        if i == n_kv:
-            project(0)
-            slot("wo0")
-    block(None, last)
-    project(1)
+        if i % 2 == 0:
+            project(i // 2 - 1)
+            slot(f"w{i // 2 - 1}")
+    block(None, len(units) - 1)
+    project(n_kv - 1)
 
     with jax.named_scope("tail"):
         seg_all().wait_send()
@@ -402,7 +423,6 @@
                 pltpu.VMEM((n_q + 2, d, NC), BF16),
                 pltpu.VMEM((hkv, 2 * n, 2, HALF, DH), BF16),
                 pltpu.VMEM((2, hq, HALF, DH), BF16),
-                pltpu.VMEM((lq, hq * DH), BF16),
                 pltpu.VMEM((2, n // 2 + 1, g_sz, KB, HALF), F32),
                 pltpu.VMEM((n + 1, KB, HALF), F32),
                 pltpu.VMEM((2, 2, g_sz, 8, HALF), F32),
@@ -413,7 +433,7 @@
                 pltpu.VMEM((hkv, DH, g_sz * HALF), F32),
                 pltpu.VMEM((n_q, lq, NC), F32),
                 pltpu.VMEM((n, 2, HALF), jnp.int32),
-                dma, dma((2 * n_q + 2 * hkv,)), dma, dma,
+                dma((2,)), dma((2 * n_q + 6,)), dma, dma,
                 dma, dma((2 * hkv,)), dma((2 * hkv,)), dma((2 * hkv,)), dma,
             ],
             compiler_params=pltpu.CompilerParams(

time: 40.1 us -> 38.9 us (0.970)
  Pallas kernels: 38.5 us -> 37.6 us
    pallas_call x1, Pallas kernels: 38.5 us -> 37.6 us  [local(): pl.pallas_call(functools.partial(_kernel, n, g_sz), out_shape=pltpu.VMEM(...]
where the time goes in v4:
time: 38.9 us
  Pallas kernels  37.6 us (97%)
  local copies, waits for them, and re-layouts  1.23 us (3%)
    pallas_call x1, Pallas kernels, local(): pl.pallas_call(functools.partial(_kernel, n, g_sz), out_shape=pltpu.VMEM(...  37.6 us
    unnamed x1, local copies, waits for them, and re-layouts  1.23 us

profile of v4, /device:TPU:0, one launch (start us, length us, event | category | flops | bytes accessed | tf_op | source)
XLA Modules:
  0.0 38.9 jit_solution(17569896784301059972)
XLA Ops:
  0.0 37.6 %layer.1 = bf16[256,3584]{1,0:T(8,128)(2,1)S(1)} custom-call(bf16[256,3584]{1,0:T(8,128)(2,1)} %x_hbm.1, s32[2,128]{1,0:T(2,128)} %bitcast.1, bf16[3584,3584]{1,0:T(8,128)(2,1)} %wq_hbm.1, bf16[3584,512]{1,0:T(8,128)(2,1)} %wk_hbm.1, bf16[3584,512]{1,0:T(8,128)(2,1)} %wv_hbm.1, bf16[3584,3584]{1,0:T(8,128)(2,1)} %wo_hbm.1), custom_call_target="tpu_custom_call" | custom-call | tf_op jit(solution)/shard_map/layer/pallas_call | solution.py:416
  37.6 1.2 %copy.8 = bf16[256,3584]{1,0:T(8,128)(2,1)} copy(bf16[256,3584]{1,0:T(8,128)(2,1)S(1)} %layer.1) | data formatting | bytes 3670016

commit v5 on v4

--- a/solution.py
+++ b/solution.py
@@ -127,8 +127,8 @@
         "q1": ([(o, 1)], []),
         "q2": ([], [(f, 1), (o, 3)]),
         "q3": ([(f, 0), (o, 2)], [(d, 0)]),
-        "q4": ([(f, 1)], [(f, 2), (o, 4)]),
-        "q5": ([(o, 3), (d, 0)], [(d, 1)]),
+        "q4": ([(f, 1)], [(f, 2)]),
+        "q5": ([(o, 3), (d, 0)], [(o, 4), (d, 1)]),
         "q6": ([(f, 2), (o, 4)], [(f, 3), (o, 5)]),
         "s0": ([(o, 5), (d, 1)], [(d, 2)]),
         "s1": ([(f, 3), (o, 6), (d, 2)], [(f, 4)]),

time: 38.9 us -> 38.8 us (level)
  no operation moved by 1% of the time
where the time goes in v5:
time: 38.8 us; the launch traced here: 38.7 us
  Pallas kernels  37.5 us (97%)
  local copies, waits for them, and re-layouts  1.23 us (3%)
    pallas_call x1, Pallas kernels, local(): pl.pallas_call(functools.partial(_kernel, n, g_sz), out_shape=pltpu.VMEM(...  37.5 us
    unnamed x1, local copies, waits for them, and re-layouts  1.23 us

profile of v5, /device:TPU:0, one launch (start us, length us, event | category | flops | bytes accessed | tf_op | source)
XLA Modules:
  0.0 38.7 jit_solution(2414685135414318264)
XLA Ops:
  0.0 37.5 %layer.1 = bf16[256,3584]{1,0:T(8,128)(2,1)S(1)} custom-call(bf16[256,3584]{1,0:T(8,128)(2,1)} %x_hbm.1, s32[2,128]{1,0:T(2,128)} %bitcast.1, bf16[3584,3584]{1,0:T(8,128)(2,1)} %wq_hbm.1, bf16[3584,512]{1,0:T(8,128)(2,1)} %wk_hbm.1, bf16[3584,512]{1,0:T(8,128)(2,1)} %wv_hbm.1, bf16[3584,3584]{1,0:T(8,128)(2,1)} %wo_hbm.1), custom_call_target="tpu_custom_call" | custom-call | tf_op jit(solution)/shard_map/layer/pallas_call | solution.py:416
  37.5 1.2 %copy.8 = bf16[256,3584]{1,0:T(8,128)(2,1)} copy(bf16[256,3584]{1,0:T(8,128)(2,1)S(1)} %layer.1) | data formatting | bytes 3670016

commit v6 on v5

--- a/solution.py
+++ b/solution.py
@@ -131,9 +131,9 @@
         "q5": ([(o, 3), (d, 0)], [(o, 4), (d, 1)]),
         "q6": ([(f, 2), (o, 4)], [(f, 3), (o, 5)]),
         "s0": ([(o, 5), (d, 1)], [(d, 2)]),
-        "s1": ([(f, 3), (o, 6), (d, 2)], [(f, 4)]),
-        "s2": ([(f, 4), (o, 7), (d, 3)], [(f, 5), (d, 3), (o, 6)]),
-        "w0": ([(f, 5), (d, 4)], [(d, 4), (o, 7)]),
+        "s1": ([(o, 6), (f, 3), (d, 2)], [(f, 4)]),
+        "s2": ([(o, 7), (f, 4), (d, 3)], [(o, 6), (f, 5), (d, 3)]),
+        "w0": ([(f, 5), (d, 4)], [(o, 7), (d, 4)]),
         "s3": ([], [(f, 6)]),
         "s4": ([(f, 6), (d, 5)], [(d, 5), (f, 7)]),
         "w1": ([(f, 7), (d, 6)], [(d, 6)]),

time: 38.8 us -> 39.9 us (1.028)
  Pallas kernels: 37.5 us -> 38.6 us
    pallas_call x1, Pallas kernels: 37.5 us -> 38.6 us  [local(): pl.pallas_call(functools.partial(_kernel, n, g_sz), out_shape=pltpu.VMEM(...]
where the time goes in v6:
time: 39.9 us; the launch traced here: 39.8 us
  Pallas kernels  38.6 us (97%)
  local copies, waits for them, and re-layouts  1.23 us (3%)
    pallas_call x1, Pallas kernels, local(): pl.pallas_call(functools.partial(_kernel, n, g_sz), out_shape=pltpu.VMEM(...  38.6 us
    unnamed x1, local copies, waits for them, and re-layouts  1.23 us

profile of v6, /device:TPU:0, one launch (start us, length us, event | category | flops | bytes accessed | tf_op | source)
XLA Modules:
  0.0 39.8 jit_solution(8472185892628889555)
XLA Ops:
  0.0 38.6 %layer.1 = bf16[256,3584]{1,0:T(8,128)(2,1)S(1)} custom-call(bf16[256,3584]{1,0:T(8,128)(2,1)} %x_hbm.1, s32[2,128]{1,0:T(2,128)} %bitcast.1, bf16[3584,3584]{1,0:T(8,128)(2,1)} %wq_hbm.1, bf16[3584,512]{1,0:T(8,128)(2,1)} %wk_hbm.1, bf16[3584,512]{1,0:T(8,128)(2,1)} %wv_hbm.1, bf16[3584,3584]{1,0:T(8,128)(2,1)} %wo_hbm.1), custom_call_target="tpu_custom_call" | custom-call | tf_op jit(solution)/shard_map/layer/pallas_call | solution.py:416
  38.6 1.2 %copy.8 = bf16[256,3584]{1,0:T(8,128)(2,1)} copy(bf16[256,3584]{1,0:T(8,128)(2,1)S(1)} %layer.1) | data formatting | bytes 3670016
